TPU v7x, 32 devices: a whole 2x2x4 slice. The times are simulated.
32 devices in a mesh: rel: 2 (over y), row: 4 (over x, core), col: 4 (over z).
Axes of the slice: x: 2, y: 2, z: 4, core: 2. Of those that a mesh axis runs over, the one named last changes fastest.
Arguments:
- features: float32 [4, 16, 256, 128], P('rel', ('row', 'col')), may hold values from -6 to 6
- lap_tiles: bfloat16 [4, 4, 4, 16, 256, 256], P('rel', 'row', 'col'), may hold values from -0.046875 to 0.046875
- tile_rows: int32 [4, 4, 4, 16], P('rel', 'row', 'col'), may hold values from 0 to 3
- tile_cols: int32 [4, 4, 4, 16], P('rel', 'row', 'col'), may hold values from 0 to 3
- tile_count: int32 [4, 4, 4], P('rel', 'row', 'col'), may hold values from 2 to 16, as said below
- cheb_coefs: float32 [4, 5], P('rel'), may hold values from -1 to 1
- merging_weight: bfloat16 [512, 128], replicated, may hold values from -0.25 to 0.25
Outputs:
- merged_rows: float32 [16, 256, 128], P(('row', 'col'), 'rel')
Inputs may be any that keep to these rules, and one draw needn't show every extreme that they name: Only the first tile_count slots of a device count; in every relation some device has 16 valid slots.
All inputs are finite; a program needn't handle non-finite values.
Results may differ from a plain program's by a relative error of at most 0.0063.
Values may be sent and summed in bfloat16 or wider, within the bound.
A program may use at most 64 MiB of HBM per device.

v0:
```python
import jax
import jax.numpy as jnp
from jax import lax
from jax.sharding import PartitionSpec as P

ORDERS = 4


def local_product(block_tiles, block_rows, block_cols, block_count, source, col_count, piece_rows):
    tile_size = block_tiles.shape[-1]
    width = source.shape[-1]
    running = jnp.zeros((col_count * piece_rows, width), jnp.float32)

    def advance(slot_index, running):
        block_tile = block_tiles[slot_index]
        start_col = block_cols[slot_index] * tile_size
        start_row = block_rows[slot_index] * tile_size
        source_rows = lax.dynamic_slice_in_dim(source, start_col, tile_size, 0)
        product = jnp.dot(block_tile, source_rows, preferred_element_type=jnp.float32)
        current = lax.dynamic_slice_in_dim(running, start_row, tile_size, 0)
        return lax.dynamic_update_slice_in_dim(running, current + product, start_row, 0)

    running = lax.fori_loop(0, block_count, advance, running)
    return running.reshape(col_count, piece_rows, width)


def local(features, lap_tiles, tile_rows, tile_cols, tile_count, cheb_coefs, merging_weight):
    col_count = lax.axis_size("col")
    rel_count = lax.axis_size("rel")
    local_rels = features.shape[0]
    piece_rows = features.shape[2]
    width = features.shape[3]
    current = features
    earlier = current
    embedding = cheb_coefs[:, 0][:, None, None, None] * current
    for degree in range(1, ORDERS + 1):
        operand = current.astype(jnp.bfloat16)
        collected = []
        for relation in range(local_rels):
            gathered = lax.all_gather(operand[relation], "row", axis=0, tiled=True)
            partial_value = local_product(
                lap_tiles[relation, 0, 0],
                tile_rows[relation, 0, 0],
                tile_cols[relation, 0, 0],
                tile_count[relation, 0, 0],
                gathered.reshape(-1, width),
                col_count,
                piece_rows,
            )
            collected.append(
                lax.psum_scatter(partial_value, "col", scatter_dimension=0, tiled=True)
            )
        applied = jnp.stack(collected)
        if degree == 1:
            following = applied
        else:
            following = 2.0 * applied - earlier
        earlier, current = (current, following)
        embedding = embedding + cheb_coefs[:, degree][:, None, None, None] * current
    embedded = embedding.astype(jnp.bfloat16)
    exchanged = lax.all_to_all(embedded, "rel", split_axis=2, concat_axis=3, tiled=True)
    grouped = merging_weight.reshape(rel_count, local_rels, width, width)
    merged_rows = jnp.zeros((exchanged.shape[2], width), jnp.float32)
    for relation in range(local_rels):
        weight_rows = grouped[:, relation].reshape(rel_count * width, width)
        merged_rows = merged_rows + jnp.dot(
            exchanged[relation, 0], weight_rows, preferred_element_type=jnp.float32
        )
    return merged_rows[None]


def solution(mesh):
    placed = (
        P("rel", ("row", "col"), None, None),
        P("rel", "row", "col", None, None, None),
        P("rel", "row", "col", None),
        P("rel", "row", "col", None),
        P("rel", "row", "col"),
        P("rel", None),
        P(),
    )
    return jax.shard_map(
        local, mesh=mesh, in_specs=placed, out_specs=P(("row", "col"), "rel", None), check_vma=False
    )
```

profile of v0, /device:TPU:0, one launch (start us, length us, event | category | flops | bytes accessed | tf_op | source)
XLA Modules:
  0.0 661.6 jit_solution(5006918419046245233)
XLA Ops:
  6.6 4.0 slice_bitcast_fusion.1
  11.2 7.2 %all-gather = bf16[4,1,256,128]{3,2,1,0:T(8,128)(2,1)S(1)} all-gather(bf16[1,1,256,128]{3,2,1,0:T(8,128)(2,1)S(1)} %get-tuple-element.446), channel_id=2, replica_groups=mesh['rel'=2,'row'=4,'col'=4] {'row'}, dimensions={0}, use_global_device_ids=true | all-gather | bytes 327680 | tf_op jit(solution)/shard_map/all_gather | solution.py:40
  18.5 67.5 %while.80 = (s32[]{:T(128)}, f32[1024,128]{1,0:T(8,128)S(1)}, s32[]{:T(128)}, s32[16]{0:T(128)S(1)}, bf16[16,256,256]{2,1,0:T(8,128)(2,1)}, /*index=5*/s32[16]{0...) while((s32[]{:T(128)}, f32[1024,128]{1,0:T(8,128)S(1)}, ...), condition=%wide.region_1.0_spmd, body=%wide.region_0.0_spmd.sunk | while | flops 16809996 | bytes 459031 | solution.py:23
  25.8 1.1 fusion.88
  59.2 1.1 fusion.88
  84.3 1.1 fusion.88
  86.9 5.8 all-gather.1
  92.7 56.8 %while.81 = (s32[]{:T(128)}, f32[1024,128]{1,0:T(8,128)S(1)}, s32[]{:T(128)}, s32[16]{0:T(128)S(1)}, bf16[16,256,256]{2,1,0:T(8,128)(2,1)S(1)}, /*index=5*/s32[1...) while((s32[]{:T(128)}, f32[1024,128]{1,0:T(8,128)S(1)}, ...), condition=%wide.region_4.0_spmd, body=%wide.region_3.0_spmd.sunk | while | flops 16809996 | bytes 459031 | solution.py:23
  150.4 21.2 %reduce-scatter.11.cloned.1.call-done = f32[1,256,128]{2,1,0:T(8,128)} async-done(((f32[4,256,128]{2,1,0:T(8,128)}), f32[1,256,128]{2,1,0:T(8,128)}) %reduce-scatter.11.cloned.1.call-update) | async-done | bytes 131088 | tf_op jit(solution)/shard_map/reduce_scatter | solution.py:51
  172.6 5.8 all-gather.2
  178.4 71.2 %while.82 = (s32[]{:T(128)}, f32[1024,128]{1,0:T(8,128)S(1)}, s32[]{:T(128)}, s32[16]{0:T(128)S(1)}, bf16[16,256,256]{2,1,0:T(8,128)(2,1)}, /*index=5*/s32[16]{0...) while((s32[]{:T(128)}, f32[1024,128]{1,0:T(8,128)S(1)}, ...), condition=%wide.region_7.0_spmd, body=%wide.region_6.0_spmd.sunk | while | flops 16809996 | bytes 459031 | solution.py:23
  199.4 1.1 fusion.94
  217.1 1.1 fusion.94
  234.7 1.1 fusion.94
  250.5 5.8 all-gather.3
  256.3 57.4 %while.83 = (s32[]{:T(128)}, f32[1024,128]{1,0:T(8,128)S(1)}, s32[]{:T(128)}, s32[16]{0:T(128)S(1)}, bf16[16,256,256]{2,1,0:T(8,128)(2,1)S(1)}, /*index=5*/s32[1...) while((s32[]{:T(128)}, f32[1024,128]{1,0:T(8,128)S(1)}, ...), condition=%wide.region_10.0_spmd, body=%wide.region_9.0_spmd.sunk | while | flops 16809996 | bytes 459031 | solution.py:23
  314.7 19.2 %reduce-scatter.15.cloned.1.call-done = f32[1,256,128]{2,1,0:T(8,128)} async-done(((f32[4,256,128]{2,1,0:T(8,128)}), f32[1,256,128]{2,1,0:T(8,128)}) %reduce-scatter.15.cloned.1.call-update) | async-done | bytes 131088 | tf_op jit(solution)/shard_map/reduce_scatter | solution.py:51
  334.9 5.8 all-gather.4
  340.7 71.2 %while.84 = (s32[]{:T(128)}, f32[1024,128]{1,0:T(8,128)S(1)}, s32[]{:T(128)}, s32[16]{0:T(128)S(1)}, bf16[16,256,256]{2,1,0:T(8,128)(2,1)}, /*index=5*/s32[16]{0...) while((s32[]{:T(128)}, f32[1024,128]{1,0:T(8,128)S(1)}, ...), condition=%wide.region_13.0_spmd, body=%wide.region_12.0_spmd.sunk | while | flops 16809996 | bytes 459031 | solution.py:23
  361.7 1.1 fusion.100
  379.3 1.1 fusion.100
  412.8 5.9 all-gather.5
  418.8 51.0 %while.85 = (s32[]{:T(128)}, f32[1024,128]{1,0:T(8,128)S(1)}, s32[]{:T(128)}, s32[16]{0:T(128)S(1)}, bf16[16,256,256]{2,1,0:T(8,128)(2,1)S(1)}, /*index=5*/s32[1...) while((s32[]{:T(128)}, f32[1024,128]{1,0:T(8,128)S(1)}, ...), condition=%wide.region_16.0_spmd, body=%wide.region_15.0_spmd.sunk | while | flops 16809996 | bytes 459031 | solution.py:23
  470.6 19.1 %reduce-scatter.19.cloned.1.call-done = f32[1,256,128]{2,1,0:T(8,128)} async-done(((f32[4,256,128]{2,1,0:T(8,128)}), f32[1,256,128]{2,1,0:T(8,128)}) %reduce-scatter.19.cloned.1.call-update) | async-done | bytes 131088 | tf_op jit(solution)/shard_map/reduce_scatter | solution.py:51
  491.4 5.8 all-gather.6
  497.2 65.7 %while.86 = (s32[]{:T(128)}, f32[1024,128]{1,0:T(8,128)S(1)}, s32[]{:T(128)}, s32[16]{0:T(128)S(1)}, bf16[16,256,256]{2,1,0:T(8,128)(2,1)}, /*index=5*/s32[16]{0...) while((s32[]{:T(128)}, f32[1024,128]{1,0:T(8,128)S(1)}, ...), condition=%wide.region_19.0_spmd, body=%wide.region_18.0_spmd.sunk | while | flops 16809996 | bytes 459031 | solution.py:23
  563.8 6.0 all-gather.7
  569.8 53.6 %while.87 = (s32[]{:T(128)}, f32[1024,128]{1,0:T(8,128)S(1)}, s32[]{:T(128)}, s32[16]{0:T(128)S(1)}, bf16[16,256,256]{2,1,0:T(8,128)(2,1)S(1)}, /*index=5*/s32[1...) while((s32[]{:T(128)}, f32[1024,128]{1,0:T(8,128)S(1)}, ...), condition=%wide.region_22.0_spmd, body=%wide.region_21.0_spmd.sunk | while | flops 16809996 | bytes 459031 | solution.py:23
  624.5 19.0 %reduce-scatter.23.cloned.1.call-done = f32[1,256,128]{2,1,0:T(8,128)} async-done(((f32[4,256,128]{2,1,0:T(8,128)}), f32[1,256,128]{2,1,0:T(8,128)}) %reduce-scatter.23.cloned.1.call-update) | async-done | bytes 131088 | tf_op jit(solution)/shard_map/reduce_scatter | solution.py:51
  643.5 1.3 fusion.46
  645.6 3.4 all-to-all-start
  649.0 4.4 all-to-all-done
  (457 shorter events, 246.2 us)
Async XLA Ops:
  6.5 4.1 copy-start.14
  6.5 4.7 copy-start.8
  6.5 11.9 %copy-start.16 = (s32[2,1,1,16]{3,2,1,0:T(1,128)S(1)}, s32[2,1,1,16]{3,2,1,0:T(1,128)}, u32[]{:S(2)}) copy-start(s32[2,1,1,16]{3,2,1,0:T(1,128)} %param.25) | copy-start | bytes 388
  6.5 11.9 %copy-start.15 = (s32[2,1,1,16]{3,2,1,0:T(1,128)S(1)}, s32[2,1,1,16]{3,2,1,0:T(1,128)}, u32[]{:S(2)}) copy-start(s32[2,1,1,16]{3,2,1,0:T(1,128)} %param.26) | copy-start | bytes 388
  6.5 143.9 %reduce-scatter.9.cloned.1.call-start = ((), (), s32[]{:S(2)}) async-start(), calls=%async_computation.9 | async-start | bytes 655360 | tf_op jit(solution)/shard_map/reduce_scatter | solution.py:51
  86.0 0.8 copy-start.1
  86.9 84.8 %reduce-scatter.11.cloned.1.call-start = ((), (), s32[]{:S(2)}) async-start(), calls=%async_computation.10 | async-start | bytes 655360 | tf_op jit(solution)/shard_map/reduce_scatter | solution.py:51
  149.5 0.8 copy-start.2
  150.4 164.3 %reduce-scatter.13.cloned.1.call-start = ((), (), s32[]{:S(2)}) async-start(), calls=%async_computation.11 | async-start | bytes 655360 | tf_op jit(solution)/shard_map/reduce_scatter | solution.py:51
  249.7 0.8 copy-start.3
  250.5 83.4 %reduce-scatter.15.cloned.1.call-start = ((), (), s32[]{:S(2)}) async-start(), calls=%async_computation.12 | async-start | bytes 655360 | tf_op jit(solution)/shard_map/reduce_scatter | solution.py:51
  313.8 0.8 copy-start.4
  314.6 156.0 %reduce-scatter.17.cloned.1.call-start = ((), (), s32[]{:S(2)}) async-start(), calls=%async_computation.13 | async-start | bytes 655360 | tf_op jit(solution)/shard_map/reduce_scatter | solution.py:51
  411.9 0.8 copy-start.5
  412.7 77.0 %copy-start.9 = (f32[1,256,128]{2,1,0:T(8,128)S(1)}, f32[1,256,128]{2,1,0:T(8,128)}, u32[]{:S(2)}) copy-start(f32[1,256,128]{2,1,0:T(8,128)} %reduce-scatter.9.cloned.1.call-done) | copy-start | bytes 393220
  412.7 77.0 %copy-start.10 = (f32[1,256,128]{2,1,0:T(8,128)S(1)}, f32[1,256,128]{2,1,0:T(8,128)}, u32[]{:S(2)}) copy-start(f32[1,256,128]{2,1,0:T(8,128)} %reduce-scatter.11.cloned.1.call-done) | copy-start | bytes 393220
  412.8 77.0 %reduce-scatter.19.cloned.1.call-start = ((), (), s32[]{:S(2)}) async-start(), calls=%async_computation.14 | async-start | bytes 655360 | tf_op jit(solution)/shard_map/reduce_scatter | solution.py:51
  469.7 0.8 copy-start.6
  470.6 153.9 %reduce-scatter.21.cloned.1.call-start = ((), (), s32[]{:S(2)}) async-start(), calls=%async_computation.15 | async-start | bytes 655360 | tf_op jit(solution)/shard_map/reduce_scatter | solution.py:51
  562.9 0.8 copy-start.7
  563.7 60.5 %copy-start.13 = (f32[2,5]{1,0:T(2,128)S(1)}, f32[2,5]{1,0:T(2,128)}, u32[]{:S(2)}) copy-start(f32[2,5]{1,0:T(2,128)} %param.28) | copy-start | bytes 124
  563.8 79.8 %copy-start.11 = (f32[1,256,128]{2,1,0:T(8,128)S(1)}, f32[1,256,128]{2,1,0:T(8,128)}, u32[]{:S(2)}) copy-start(f32[1,256,128]{2,1,0:T(8,128)} %reduce-scatter.13.cloned.1.call-done) | copy-start | bytes 393220
  563.8 79.7 %reduce-scatter.23.cloned.1.call-start = ((), (), s32[]{:S(2)}) async-start(), calls=%async_computation.16 | async-start | bytes 655360 | tf_op jit(solution)/shard_map/reduce_scatter | solution.py:51
  623.4 0.8 copy-start
  623.4 25.6 %copy-start.12 = (bf16[512,128]{1,0:T(8,128)(2,1)S(1)}, bf16[512,128]{1,0:T(8,128)(2,1)}, u32[]{:S(2)}) copy-start(bf16[512,128]{1,0:T(8,128)(2,1)} %param.29) | copy-start | bytes 393220
  645.6 7.8 %all-to-all-start = ((bf16[2,1,256,128]{3,0,1,2:T(2,128)(2,1)}), bf16[2,1,256,128]{3,0,1,2:T(2,128)(2,1)S(1)}, u32[]{:S(2)}, u32[]{:S(2)}) async-start(bf16[2,1,256,128]{3,0,1,2:T(2,128)(2,1)} %copy.12), calls=%async_computation.8 | async-start | bytes 262144 | tf_op jit(solution)/shard_map/all_to_all | solution.py:61
Sparse Core Ops, SparseCore 0:
  87.0 22.1 reduce-scatter.8
  150.5 21.0 reduce-scatter.10
  250.6 20.0 reduce-scatter.12
  314.7 19.1 reduce-scatter.14
  412.9 20.0 reduce-scatter.16
  470.7 19.0 reduce-scatter.18
  563.9 20.1 reduce-scatter.20
  624.4 19.0 reduce-scatter.22
where the time goes:
time: 668 us; the launch traced here: 662 us
  loops' own time  253 us (38%)
  local copies, waits for them, and re-layouts  174 us (26%)
  waiting for transfers between devices  83.2 us (12%)
  matrix products  81.7 us (12%)
  blocking collectives  48 us (7%)
  between operations  13.8 us (2%)
    another operation x8, loops' own time, local_product(): running = lax.fori_loop(0, block_count, advance, running)  253 us
    dot_general x128, matrix products, advance(): jnp.dot(block_tile, source_rows, preferred_element_type=jnp.float32)  80.7 us
    dynamic_slice x128, local copies, waits for them, and re-layouts, advance(): start_row = block_rows[slot_index] * tile_size  80.4 us
    dynamic_slice x128, local copies, waits for them, and re-layouts, advance(): start_col = block_cols[slot_index] * tile_size  80.1 us
    reduce_scatter x8, waiting for transfers between devices, local(): lax.psum_scatter(partial_value, 'col', scatter_dimension=0, tiled=True)  78.6 us
    all_gather x8, blocking collectives, local(): gathered = lax.all_gather(operand[relation], 'row', axis=0, tiled=True)  48 us
  transfers between devices with their start and end apart: 9, of which 5 were waited for; matrix products, arithmetic and copies ran while one was open for 14% of the time, Pallas kernels for 0%

commit v1 on v0

v1 whole, which is shorter than its diff:
```python
import functools

import jax
import jax.numpy as jnp
from jax import lax
from jax.experimental import pallas as pl
from jax.experimental.pallas import tpu as pltpu
from jax.sharding import PartitionSpec as P

ORDERS = 4
MESH = pl.DeviceIdType.MESH
VMEM_LIMIT = 60 * 1024 * 1024


def assemble_kernel(rows_ref, cols_ref, count_ref, tiles_ref, dense_ref, acc_ref):
    relation, block = pl.program_id(0), pl.program_id(1)
    slots, tile = tiles_ref.shape[1], tiles_ref.shape[2]
    acc_ref[...] = jnp.zeros_like(acc_ref)

    def add_slot(slot, carry):
        @pl.when((slot < count_ref[relation]) & (rows_ref[relation, slot] == block))
        def _():
            col = cols_ref[relation, slot]
            acc_ref[col] += tiles_ref[0, slot].astype(jnp.float32)

        return carry

    lax.fori_loop(0, slots, add_slot, 0)
    for col in range(acc_ref.shape[0]):
        dense_ref[0, 0, :, col * tile : (col + 1) * tile] = acc_ref[col].astype(dense_ref.dtype)


def assemble(lap_tiles, tile_rows, tile_cols, tile_count, row_count, col_count):
    rels, slots, tile, _ = lap_tiles.shape
    return pl.pallas_call(
        assemble_kernel,
        grid=(rels, col_count),
        out_shape=jax.ShapeDtypeStruct((rels, col_count, tile, row_count * tile), lap_tiles.dtype),
        in_specs=[
            pl.BlockSpec(memory_space=pltpu.SMEM),
            pl.BlockSpec(memory_space=pltpu.SMEM),
            pl.BlockSpec(memory_space=pltpu.SMEM),
            pl.BlockSpec((1, slots, tile, tile), lambda r, b: (r, 0, 0, 0)),
        ],
        out_specs=pl.BlockSpec((1, 1, tile, row_count * tile), lambda r, b: (r, b, 0, 0)),
        scratch_shapes=[pltpu.VMEM((row_count, tile, tile), jnp.float32)],
        compiler_params=pltpu.CompilerParams(vmem_limit_bytes=24 * 1024 * 1024),
    )(tile_rows, tile_cols, tile_count, lap_tiles)


def span(count, body, unroll_up_to=4):
    if count <= unroll_up_to:
        for index in range(count):
            body(index)
    else:
        lax.fori_loop(0, count, lambda index, carry: (body(index), carry)[1], 0)


def propagate_kernel(
    row_count, col_count, rel_count,
    features_ref, dense_ref, coefs_ref, weight_ref, merged_ref,
    lap_ref, gather_ref, partial_ref, arrived_ref, own_ref, current_ref, earlier_ref, total_ref,
    embed_ref, exchange_ref,
    load_sem, gather_send, gather_recv, scatter_send, scatter_recv, exchange_send, exchange_recv,
):
    rels, _, piece_rows, width = features_ref.shape
    my_row, my_col, my_rel = lax.axis_index("row"), lax.axis_index("col"), lax.axis_index("rel")
    part = piece_rows // rel_count

    def peer(me, offset, count):
        return lax.rem(me + offset, count)

    loads = [
        pltpu.make_async_copy(dense_ref.at[r], lap_ref.at[r], load_sem.at[r]) for r in range(rels)
    ]
    for load in loads:
        load.start()

    barrier = pltpu.get_barrier_semaphore()
    for axis, me, count in (("row", my_row, row_count), ("col", my_col, col_count), ("rel", my_rel, rel_count)):
        for offset in range(1, count):
            pl.semaphore_signal(
                barrier, inc=1, device_id={axis: peer(me, offset, count)}, device_id_type=MESH
            )
    pl.semaphore_wait(barrier, row_count + col_count + rel_count - 3)

    def gather_copy(order, r, source, target):
        return pltpu.make_async_remote_copy(
            src_ref=gather_ref.at[order, r, pl.ds(pl.multiple_of(source * piece_rows, piece_rows), piece_rows)],
            dst_ref=gather_ref.at[order, r, pl.ds(pl.multiple_of(source * piece_rows, piece_rows), piece_rows)],
            send_sem=gather_send.at[order, r, target],
            recv_sem=gather_recv.at[order, r, source],
            device_id={"row": target},
            device_id_type=MESH,
        )

    def scatter_copy(order, r, source, target):
        return pltpu.make_async_remote_copy(
            src_ref=partial_ref.at[order, r, target],
            dst_ref=arrived_ref.at[order, r, source],
            send_sem=scatter_send.at[order, r, target],
            recv_sem=scatter_recv.at[order, r, source],
            device_id={"col": target},
            device_id_type=MESH,
        )

    def exchange_copy(r, source, target):
        return pltpu.make_async_remote_copy(
            src_ref=embed_ref.at[r, target],
            dst_ref=exchange_ref.at[source, r],
            send_sem=exchange_send.at[r, target],
            recv_sem=exchange_recv.at[r, source],
            device_id={"rel": target},
            device_id_type=MESH,
        )

    def send_operand(order, r, value):
        gather_ref[order, r, pl.ds(pl.multiple_of(my_row * piece_rows, piece_rows), piece_rows)] = (
            value.astype(gather_ref.dtype)
        )
        for offset in range(1, row_count):
            gather_copy(order, r, my_row, peer(my_row, offset, row_count)).start()

    for r in range(rels):
        value = features_ref[r, 0]
        send_operand(0, r, value)
        current_ref[r] = value
        earlier_ref[r] = jnp.zeros_like(value)
        total_ref[r] = coefs_ref[r, 0] * value
    for load in loads:
        load.wait()

    def product(order, r, block):
        return jnp.dot(lap_ref[r, block], gather_ref[order, r], preferred_element_type=jnp.float32)

    def one_order(order, carry):
        for r in range(rels):
            for offset in range(1, row_count):
                gather_copy(order, r, peer(my_row, offset, row_count), my_row).wait_recv()

            def push(index):
                block = peer(my_col, index + 1, col_count)
                partial_ref[order, r, block] = product(order, r, block).astype(partial_ref.dtype)
                scatter_copy(order, r, my_col, block).start()

            span(col_count - 1, push)
            own_ref[r] = product(order, r, my_col)
        scale = jnp.where(order == 0, 1.0, 2.0).astype(jnp.float32)
        for r in range(rels):
            applied = own_ref[r]
            for offset in range(1, col_count):
                source = peer(my_col, offset, col_count)
                scatter_copy(order, r, source, my_col).wait_recv()
                applied = applied + arrived_ref[order, r, source].astype(jnp.float32)
            following = scale * applied - earlier_ref[r]

            @pl.when(order + 1 < ORDERS)
            def _():
                send_operand(order + 1, r, following)

            earlier_ref[r] = current_ref[r]
            current_ref[r] = following
            total_ref[r] += coefs_ref[r, order + 1] * following
        return carry

    lax.fori_loop(0, ORDERS, one_order, 0)

    for r in range(rels):
        embedded = total_ref[r].astype(embed_ref.dtype)
        embed_ref[r] = embedded.reshape(rel_count, part, width)
        exchange_ref[my_rel, r] = embed_ref[r, my_rel]
        for offset in range(1, rel_count):
            exchange_copy(r, my_rel, peer(my_rel, offset, rel_count)).start()

    def drain(order, carry):
        for r in range(rels):
            for offset in range(1, row_count):
                gather_copy(order, r, my_row, peer(my_row, offset, row_count)).wait_send()
            for offset in range(1, col_count):
                scatter_copy(order, r, my_col, peer(my_col, offset, col_count)).wait_send()
        return carry

    lax.fori_loop(0, ORDERS, drain, 0)
    for r in range(rels):
        for offset in range(1, rel_count):
            other = peer(my_rel, offset, rel_count)
            exchange_copy(r, my_rel, other).wait_send()
            exchange_copy(r, other, my_rel).wait_recv()
    merged = jnp.zeros((part, width), jnp.float32)
    for group in range(rel_count):
        for r in range(rels):
            start = (group * rels + r) * width
            merged = merged + jnp.dot(
                exchange_ref[group, r], weight_ref[start : start + width, :],
                preferred_element_type=jnp.float32,
            )
    merged_ref[0] = merged


def local(features, lap_tiles, tile_rows, tile_cols, tile_count, cheb_coefs, merging_weight):
    row_count, col_count, rel_count = (lax.axis_size(name) for name in ("row", "col", "rel"))
    rels, _, piece_rows, width = features.shape
    part = piece_rows // rel_count
    dense = assemble(
        lap_tiles[:, 0, 0], tile_rows[:, 0, 0], tile_cols[:, 0, 0], tile_count[:, 0, 0], row_count, col_count
    )
    vmem = pl.BlockSpec(memory_space=pltpu.VMEM)
    half = jnp.bfloat16
    dma = pltpu.SemaphoreType.DMA
    return pl.pallas_call(
        functools.partial(propagate_kernel, row_count, col_count, rel_count),
        out_shape=jax.ShapeDtypeStruct((1, part, width), jnp.float32),
        in_specs=[vmem, pl.BlockSpec(memory_space=pl.ANY), pl.BlockSpec(memory_space=pltpu.SMEM), vmem],
        out_specs=vmem,
        scratch_shapes=[
            pltpu.VMEM(dense.shape, dense.dtype),
            pltpu.VMEM((ORDERS, rels, row_count * piece_rows, width), half),
            pltpu.VMEM((ORDERS, rels, col_count, piece_rows, width), half),
            pltpu.VMEM((ORDERS, rels, col_count, piece_rows, width), half),
            pltpu.VMEM((rels, piece_rows, width), jnp.float32),
            pltpu.VMEM((rels, piece_rows, width), jnp.float32),
            pltpu.VMEM((rels, piece_rows, width), jnp.float32),
            pltpu.VMEM((rels, piece_rows, width), jnp.float32),
            pltpu.VMEM((rels, rel_count, part, width), half),
            pltpu.VMEM((rel_count, rels, part, width), half),
            dma((rels,)),
            dma((ORDERS, rels, row_count)),
            dma((ORDERS, rels, row_count)),
            dma((ORDERS, rels, col_count)),
            dma((ORDERS, rels, col_count)),
            dma((rels, rel_count)),
            dma((rels, rel_count)),
        ],
        compiler_params=pltpu.CompilerParams(
            collective_id=0, has_side_effects=True, vmem_limit_bytes=VMEM_LIMIT
        ),
    )(features, dense, cheb_coefs, merging_weight)


def solution(mesh):
    placed = (
        P("rel", ("row", "col"), None, None),
        P("rel", "row", "col", None, None, None),
        P("rel", "row", "col", None),
        P("rel", "row", "col", None),
        P("rel", "row", "col"),
        P("rel", None),
        P(),
    )
    return jax.shard_map(
        local, mesh=mesh, in_specs=placed, out_specs=P(("row", "col"), "rel", None), check_vma=False
    )
```

time: 668 us -> 82.7 us (0.12)
  loops' own time: 253 us -> 0 us
  local copies, waits for them, and re-layouts: 174 us -> 7.6 us
  waiting for transfers between devices: 83.2 us -> 0 us
  matrix products: 81.7 us -> 0 us
  Pallas kernels: 0 us -> 74.9 us
  blocking collectives: 48 us -> 0 us
  between operations: 13.8 us -> 0.03 us
    another operation x8 -> x0, loops' own time: 253 us -> none  [local_product(): running = lax.fori_loop(0, block_count, advance, running)]
    dynamic_slice x256 -> x0, local copies, waits for them, and re-layouts: 161 us -> none  [the longest x128 80.4 us: advance(): start_row = block_rows[slot_index] * tile_size]
    dot_general x130 -> x0, matrix products: 81.7 us -> none  [the longest x128 80.7 us: advance(): jnp.dot(block_tile, source_rows, preferred_element_type=jnp.float32)]
    reduce_scatter x8 -> x0, waiting for transfers between devices: 78.6 us -> none  [local(): lax.psum_scatter(partial_value, 'col', scatter_dimension=0, tiled=True)]
    pallas_call x0 -> x2, Pallas kernels: none -> 74.9 us  [the longest x1 70.8 us: local(): pl.pallas_call(functools.partial(propagate_kernel, row_count, col_count,...]
    all_gather x8 -> x0, blocking collectives: 48 us -> none  [local(): gathered = lax.all_gather(operand[relation], 'row', axis=0, tiled=True)]
  transfers between devices with their start and end apart: 9 -> 0, of which waited for: 5 -> 0; matrix products, arithmetic and copies ran while one was open for 14% -> 0% of each run, Pallas kernels for 0% -> 0%
where the time goes in v1:
time: 82.7 us; the launch traced here: 82.5 us
  Pallas kernels  74.9 us (91%)
  local copies, waits for them, and re-layouts  7.6 us (9%)
    pallas_call x1, Pallas kernels, local(): pl.pallas_call(functools.partial(propagate_kernel, row_count, col_count,...  70.8 us
    unnamed x11, local copies, waits for them, and re-layouts  7.6 us
    pallas_call x1, Pallas kernels, assemble(): pl.pallas_call(assemble_kernel, grid=(rels, col_count), out_shape=jax.Sha...  4.12 us

profile of v1, /device:TPU:0, one launch (start us, length us, event | category | flops | bytes accessed | tf_op | source)
XLA Modules:
  0.0 82.5 jit_solution(13154926549521738920)
XLA Ops:
  0.0 0.0 copy-start.1
  0.0 2.2 %copy-done.1 = bf16[2,1,1,16,256,256]{5,4,3,2,1,0:T(8,128)(2,1)S(1)} copy-done((bf16[2,1,1,16,256,256]{5,4,3,2,1,0:T(8,128)(2,1)S(1)}, bf16[2,1,1,16,256,256]{5,4,3,2,1,0:T(8,128)(2,1)}, u32[]{:S(2)}) %copy-start.1) | copy-done | bytes 4194328
  2.2 0.0 copy-start.2
  2.2 0.7 copy-done.2
  2.9 0.0 copy-start.3
  2.9 0.7 copy-done.3
  3.5 0.0 copy-start.4
  3.5 0.7 copy-done.4
  4.2 4.1 %shard_map.73.dense_ref = bf16[2,4,256,1024]{3,2,1,0:T(8,128)(2,1)S(1)} custom-call(s32[2,16]{1,0:T(2,128)S(1)} %bitcast.5, s32[2,16]{1,0:T(2,128)S(1)} %bitcast.6, s32[2]{0:T(128)S(1)} %bitcast.7, bf16[2,16,256,256]{3,2,1,0:T(8,128)(2,1)S(1)} %bitcast.4), custom_call_target="tpu_custom_call" | custom-call | tf_op jit(solution)/shard_map/pallas_call | solution.py:35
  8.3 0.0 copy-start
  8.3 1.9 %copy-done = bf16[2,4,256,1024]{3,2,1,0:T(8,128)(2,1)} copy-done((bf16[2,4,256,1024]{3,2,1,0:T(8,128)(2,1)}, bf16[2,4,256,1024]{3,2,1,0:T(8,128)(2,1)S(1)}, u32[]{:S(2)}) %copy-start) | copy-done | bytes 4194328
  10.3 70.8 %shard_map.74 = f32[1,128,128]{2,1,0:T(8,128)} custom-call(f32[2,1,256,128]{3,2,1,0:T(8,128)} %features_ref.1, bf16[2,4,256,1024]{3,2,1,0:T(8,128)(2,1)} %copy-done, f32[2,5]{1,0:T(2,128)} %coefs_ref.1, bf16[512,128]{1,0:T(8,128)(2,1)} %weight_ref.1), custom_call_target="tpu_custom_call" | custom-call | tf_op jit(solution)/shard_map/pallas_call | solution.py:210
  81.1 1.5 %copy.9 = f32[1,128,128]{2,1,0:T(8,128)} copy(f32[1,128,128]{2,1,0:T(8,128)} %shard_map.74) | data formatting | bytes 131072
Async XLA Ops:
  0.0 2.2 %copy-start.1 = (bf16[2,1,1,16,256,256]{5,4,3,2,1,0:T(8,128)(2,1)S(1)}, bf16[2,1,1,16,256,256]{5,4,3,2,1,0:T(8,128)(2,1)}, u32[]{:S(2)}) copy-start(bf16[2,1,1,16,256,256]{5,4,3,2,1,0:T(8,128)(2,1)} %param.8) | copy-start | bytes 12582916
  2.2 0.7 copy-start.2
  2.9 0.7 copy-start.3
  3.5 0.7 copy-start.4
  8.3 1.9 %copy-start = (bf16[2,4,256,1024]{3,2,1,0:T(8,128)(2,1)}, bf16[2,4,256,1024]{3,2,1,0:T(8,128)(2,1)S(1)}, u32[]{:S(2)}) copy-start(bf16[2,4,256,1024]{3,2,1,0:T(8,128)(2,1)S(1)} %shard_map.73.dense_ref) | copy-start | bytes 12582916

commit v2 on v1

--- a/solution.py
+++ b/solution.py
@@ -58,10 +58,10 @@
 
 def propagate_kernel(
     row_count, col_count, rel_count,
-    features_ref, dense_ref, coefs_ref, weight_ref, merged_ref,
-    lap_ref, gather_ref, partial_ref, arrived_ref, own_ref, current_ref, earlier_ref, total_ref,
+    features_hbm, dense_ref, coefs_ref, weight_hbm, merged_ref,
+    features_ref, weight_ref, lap_ref, gather_ref, partial_ref, arrived_ref, own_ref, current_ref, earlier_ref, total_ref,
     embed_ref, exchange_ref,
-    load_sem, gather_send, gather_recv, scatter_send, scatter_recv, exchange_send, exchange_recv,
+    load_sem, features_sem, weight_sem, gather_send, gather_recv, scatter_send, scatter_recv, exchange_send, exchange_recv,
 ):
     rels, _, piece_rows, width = features_ref.shape
     my_row, my_col, my_rel = lax.axis_index("row"), lax.axis_index("col"), lax.axis_index("rel")
@@ -70,11 +70,15 @@
     def peer(me, offset, count):
         return lax.rem(me + offset, count)
 
+    features_load = pltpu.make_async_copy(features_hbm, features_ref, features_sem)
+    features_load.start()
     loads = [
         pltpu.make_async_copy(dense_ref.at[r], lap_ref.at[r], load_sem.at[r]) for r in range(rels)
     ]
     for load in loads:
         load.start()
+    weight_load = pltpu.make_async_copy(weight_hbm, weight_ref, weight_sem)
+    weight_load.start()
 
     barrier = pltpu.get_barrier_semaphore()
     for axis, me, count in (("row", my_row, row_count), ("col", my_col, col_count), ("rel", my_rel, rel_count)):
@@ -121,51 +125,59 @@
         for offset in range(1, row_count):
             gather_copy(order, r, my_row, peer(my_row, offset, row_count)).start()
 
+    features_load.wait()
+    for r in range(rels):
+        send_operand(0, r, features_ref[r, 0])
     for r in range(rels):
         value = features_ref[r, 0]
-        send_operand(0, r, value)
         current_ref[r] = value
         earlier_ref[r] = jnp.zeros_like(value)
         total_ref[r] = coefs_ref[r, 0] * value
-    for load in loads:
-        load.wait()
 
     def product(order, r, block):
         return jnp.dot(lap_ref[r, block], gather_ref[order, r], preferred_element_type=jnp.float32)
 
+    def push_partials(order, r):
+        for offset in range(1, row_count):
+            gather_copy(order, r, peer(my_row, offset, row_count), my_row).wait_recv()
+
+        def push(index):
+            offset = 1 + (col_count // 2 - 1 + index) % (col_count - 1)
+            block = peer(my_col, offset, col_count)
+            partial_ref[order, r, block] = product(order, r, block).astype(partial_ref.dtype)
+            scatter_copy(order, r, my_col, block).start()
+
+        span(col_count - 1, push)
+        own_ref[r] = product(order, r, my_col)
+
+    def advance(order, r, send):
+        applied = own_ref[r]
+        for offset in range(1, col_count):
+            source = peer(my_col, offset, col_count)
+            scatter_copy(order, r, source, my_col).wait_recv()
+            applied = applied + arrived_ref[order, r, source].astype(jnp.float32)
+        scale = jnp.where(order == 0, 1.0, 2.0).astype(jnp.float32)
+        following = scale * applied - earlier_ref[r]
+        if send:
+            send_operand(order + 1, r, following)
+        earlier_ref[r] = current_ref[r]
+        current_ref[r] = following
+        total_ref[r] += coefs_ref[r, order + 1] * following
+
+    for r in range(rels):
+        loads[r].wait()
+        push_partials(0, r)
+
     def one_order(order, carry):
         for r in range(rels):
-            for offset in range(1, row_count):
-                gather_copy(order, r, peer(my_row, offset, row_count), my_row).wait_recv()
-
-            def push(index):
-                block = peer(my_col, index + 1, col_count)
-                partial_ref[order, r, block] = product(order, r, block).astype(partial_ref.dtype)
-                scatter_copy(order, r, my_col, block).start()
-
-            span(col_count - 1, push)
-            own_ref[r] = product(order, r, my_col)
-        scale = jnp.where(order == 0, 1.0, 2.0).astype(jnp.float32)
-        for r in range(rels):
-            applied = own_ref[r]
-            for offset in range(1, col_count):
-                source = peer(my_col, offset, col_count)
-                scatter_copy(order, r, source, my_col).wait_recv()
-                applied = applied + arrived_ref[order, r, source].astype(jnp.float32)
-            following = scale * applied - earlier_ref[r]
-
-            @pl.when(order + 1 < ORDERS)
-            def _():
-                send_operand(order + 1, r, following)
-
-            earlier_ref[r] = current_ref[r]
-            current_ref[r] = following
-            total_ref[r] += coefs_ref[r, order + 1] * following
+            advance(order, r, True)
+            push_partials(order + 1, r)
         return carry
 
-    lax.fori_loop(0, ORDERS, one_order, 0)
-
-    for r in range(rels):
+    lax.fori_loop(0, ORDERS - 1, one_order, 0)
+
+    for r in range(rels):
+        advance(ORDERS - 1, r, False)
         embedded = total_ref[r].astype(embed_ref.dtype)
         embed_ref[r] = embedded.reshape(rel_count, part, width)
         exchange_ref[my_rel, r] = embed_ref[r, my_rel]
@@ -186,6 +198,7 @@
             other = peer(my_rel, offset, rel_count)
             exchange_copy(r, my_rel, other).wait_send()
             exchange_copy(r, other, my_rel).wait_recv()
+    weight_load.wait()
     merged = jnp.zeros((part, width), jnp.float32)
     for group in range(rel_count):
         for r in range(rels):
@@ -205,14 +218,17 @@
         lap_tiles[:, 0, 0], tile_rows[:, 0, 0], tile_cols[:, 0, 0], tile_count[:, 0, 0], row_count, col_count
     )
     vmem = pl.BlockSpec(memory_space=pltpu.VMEM)
+    anywhere = pl.BlockSpec(memory_space=pl.ANY)
     half = jnp.bfloat16
     dma = pltpu.SemaphoreType.DMA
     return pl.pallas_call(
         functools.partial(propagate_kernel, row_count, col_count, rel_count),
         out_shape=jax.ShapeDtypeStruct((1, part, width), jnp.float32),
-        in_specs=[vmem, pl.BlockSpec(memory_space=pl.ANY), pl.BlockSpec(memory_space=pltpu.SMEM), vmem],
+        in_specs=[anywhere, anywhere, pl.BlockSpec(memory_space=pltpu.SMEM), anywhere],
         out_specs=vmem,
         scratch_shapes=[
+            pltpu.VMEM(features.shape, features.dtype),
+            pltpu.VMEM(merging_weight.shape, merging_weight.dtype),
             pltpu.VMEM(dense.shape, dense.dtype),
             pltpu.VMEM((ORDERS, rels, row_count * piece_rows, width), half),
             pltpu.VMEM((ORDERS, rels, col_count, piece_rows, width), half),
@@ -224,6 +240,8 @@
             pltpu.VMEM((rels, rel_count, part, width), half),
             pltpu.VMEM((rel_count, rels, part, width), half),
             dma((rels,)),
+            dma,
+            dma,
             dma((ORDERS, rels, row_count)),
             dma((ORDERS, rels, row_count)),
             dma((ORDERS, rels, col_count)),

time: 82.7 us -> 79.7 us (0.964)
  Pallas kernels: 74.9 us -> 71.6 us
    pallas_call x1, Pallas kernels: 70.8 us -> 67.5 us  [local(): pl.pallas_call(functools.partial(propagate_kernel, row_count, col_count,...]
where the time goes in v2:
time: 79.7 us; the launch traced here: 79.2 us
  Pallas kernels  71.6 us (90%)
  local copies, waits for them, and re-layouts  7.6 us (10%)
    pallas_call x1, Pallas kernels, local(): pl.pallas_call(functools.partial(propagate_kernel, row_count, col_count,...  67.5 us
    unnamed x11, local copies, waits for them, and re-layouts  7.6 us
    pallas_call x1, Pallas kernels, assemble(): pl.pallas_call(assemble_kernel, grid=(rels, col_count), out_shape=jax.Sha...  4.12 us

profile of v2, /device:TPU:0, one launch (start us, length us, event | category | flops | bytes accessed | tf_op | source)
XLA Modules:
  0.0 79.2 jit_solution(17412432112910010862)
XLA Ops:
  0.0 0.0 copy-start.1
  0.0 2.2 %copy-done.1 = bf16[2,1,1,16,256,256]{5,4,3,2,1,0:T(8,128)(2,1)S(1)} copy-done((bf16[2,1,1,16,256,256]{5,4,3,2,1,0:T(8,128)(2,1)S(1)}, bf16[2,1,1,16,256,256]{5,4,3,2,1,0:T(8,128)(2,1)}, u32[]{:S(2)}) %copy-start.1) | copy-done | bytes 4194328
  2.2 0.0 copy-start.2
  2.2 0.7 copy-done.2
  2.9 0.0 copy-start.3
  2.9 0.7 copy-done.3
  3.5 0.0 copy-start.4
  3.5 0.7 copy-done.4
  4.2 4.1 %shard_map.73.dense_ref = bf16[2,4,256,1024]{3,2,1,0:T(8,128)(2,1)S(1)} custom-call(s32[2,16]{1,0:T(2,128)S(1)} %bitcast.5, s32[2,16]{1,0:T(2,128)S(1)} %bitcast.6, s32[2]{0:T(128)S(1)} %bitcast.7, bf16[2,16,256,256]{3,2,1,0:T(8,128)(2,1)S(1)} %bitcast.4), custom_call_target="tpu_custom_call" | custom-call | tf_op jit(solution)/shard_map/pallas_call | solution.py:35
  8.3 0.0 copy-start
  8.3 1.9 %copy-done = bf16[2,4,256,1024]{3,2,1,0:T(8,128)(2,1)} copy-done((bf16[2,4,256,1024]{3,2,1,0:T(8,128)(2,1)}, bf16[2,4,256,1024]{3,2,1,0:T(8,128)(2,1)S(1)}, u32[]{:S(2)}) %copy-start) | copy-done | bytes 4194328
  10.3 67.5 %shard_map.74 = f32[1,128,128]{2,1,0:T(8,128)} custom-call(f32[2,1,256,128]{3,2,1,0:T(8,128)} %features_hbm.1, bf16[2,4,256,1024]{3,2,1,0:T(8,128)(2,1)} %copy-done, f32[2,5]{1,0:T(2,128)} %coefs_ref.1, bf16[512,128]{1,0:T(8,128)(2,1)} %weight_hbm.1), custom_call_target="tpu_custom_call" | custom-call | tf_op jit(solution)/shard_map/pallas_call | solution.py:224
  77.7 1.5 %copy.9 = f32[1,128,128]{2,1,0:T(8,128)} copy(f32[1,128,128]{2,1,0:T(8,128)} %shard_map.74) | data formatting | bytes 131072
Async XLA Ops:
  0.0 2.2 %copy-start.1 = (bf16[2,1,1,16,256,256]{5,4,3,2,1,0:T(8,128)(2,1)S(1)}, bf16[2,1,1,16,256,256]{5,4,3,2,1,0:T(8,128)(2,1)}, u32[]{:S(2)}) copy-start(bf16[2,1,1,16,256,256]{5,4,3,2,1,0:T(8,128)(2,1)} %param.8) | copy-start | bytes 12582916
  2.2 0.7 copy-start.2
  2.9 0.7 copy-start.3
  3.5 0.7 copy-start.4
  8.3 1.9 %copy-start = (bf16[2,4,256,1024]{3,2,1,0:T(8,128)(2,1)}, bf16[2,4,256,1024]{3,2,1,0:T(8,128)(2,1)S(1)}, u32[]{:S(2)}) copy-start(bf16[2,4,256,1024]{3,2,1,0:T(8,128)(2,1)S(1)} %shard_map.73.dense_ref) | copy-start | bytes 12582916

commit v3 on v2

--- a/solution.py
+++ b/solution.py
@@ -12,8 +12,24 @@
 VMEM_LIMIT = 60 * 1024 * 1024
 
 
-def assemble_kernel(rows_ref, cols_ref, count_ref, tiles_ref, dense_ref, acc_ref):
+def assemble_kernel(
+    rows_hbm, cols_hbm, count_hbm, tiles_ref, dense_ref, acc_ref, rows_ref, cols_ref, count_ref, index_sem
+):
     relation, block = pl.program_id(0), pl.program_id(1)
+
+    @pl.when((relation == 0) & (block == 0))
+    def _():
+        loads = [
+            pltpu.make_async_copy(source, target, index_sem.at[index])
+            for index, (source, target) in enumerate(
+                ((rows_hbm, rows_ref), (cols_hbm, cols_ref), (count_hbm, count_ref))
+            )
+        ]
+        for load in loads:
+            load.start()
+        for load in loads:
+            load.wait()
+
     slots, tile = tiles_ref.shape[1], tiles_ref.shape[2]
     acc_ref[...] = jnp.zeros_like(acc_ref)
 
@@ -37,13 +53,19 @@
         grid=(rels, col_count),
         out_shape=jax.ShapeDtypeStruct((rels, col_count, tile, row_count * tile), lap_tiles.dtype),
         in_specs=[
-            pl.BlockSpec(memory_space=pltpu.SMEM),
-            pl.BlockSpec(memory_space=pltpu.SMEM),
-            pl.BlockSpec(memory_space=pltpu.SMEM),
+            pl.BlockSpec(memory_space=pl.ANY),
+            pl.BlockSpec(memory_space=pl.ANY),
+            pl.BlockSpec(memory_space=pl.ANY),
             pl.BlockSpec((1, slots, tile, tile), lambda r, b: (r, 0, 0, 0)),
         ],
         out_specs=pl.BlockSpec((1, 1, tile, row_count * tile), lambda r, b: (r, b, 0, 0)),
-        scratch_shapes=[pltpu.VMEM((row_count, tile, tile), jnp.float32)],
+        scratch_shapes=[
+            pltpu.VMEM((row_count, tile, tile), jnp.float32),
+            pltpu.SMEM(tile_rows.shape, tile_rows.dtype),
+            pltpu.SMEM(tile_cols.shape, tile_cols.dtype),
+            pltpu.SMEM(tile_count.shape, tile_count.dtype),
+            pltpu.SemaphoreType.DMA((3,)),
+        ],
         compiler_params=pltpu.CompilerParams(vmem_limit_bytes=24 * 1024 * 1024),
     )(tile_rows, tile_cols, tile_count, lap_tiles)
 
@@ -58,10 +80,10 @@
 
 def propagate_kernel(
     row_count, col_count, rel_count,
-    features_hbm, dense_ref, coefs_ref, weight_hbm, merged_ref,
-    features_ref, weight_ref, lap_ref, gather_ref, partial_ref, arrived_ref, own_ref, current_ref, earlier_ref, total_ref,
+    features_hbm, dense_ref, coefs_hbm, weight_hbm, merged_ref,
+    coefs_ref, features_ref, weight_ref, lap_ref, gather_ref, partial_ref, arrived_ref, own_ref, current_ref, earlier_ref, total_ref,
     embed_ref, exchange_ref,
-    load_sem, features_sem, weight_sem, gather_send, gather_recv, scatter_send, scatter_recv, exchange_send, exchange_recv,
+    load_sem, coefs_sem, features_sem, weight_sem, gather_send, gather_recv, scatter_send, scatter_recv, exchange_send, exchange_recv,
 ):
     rels, _, piece_rows, width = features_ref.shape
     my_row, my_col, my_rel = lax.axis_index("row"), lax.axis_index("col"), lax.axis_index("rel")
@@ -72,6 +94,8 @@
 
     features_load = pltpu.make_async_copy(features_hbm, features_ref, features_sem)
     features_load.start()
+    coefs_load = pltpu.make_async_copy(coefs_hbm, coefs_ref, coefs_sem)
+    coefs_load.start()
     loads = [
         pltpu.make_async_copy(dense_ref.at[r], lap_ref.at[r], load_sem.at[r]) for r in range(rels)
     ]
@@ -128,6 +152,7 @@
     features_load.wait()
     for r in range(rels):
         send_operand(0, r, features_ref[r, 0])
+    coefs_load.wait()
     for r in range(rels):
         value = features_ref[r, 0]
         current_ref[r] = value
@@ -224,9 +249,10 @@
     return pl.pallas_call(
         functools.partial(propagate_kernel, row_count, col_count, rel_count),
         out_shape=jax.ShapeDtypeStruct((1, part, width), jnp.float32),
-        in_specs=[anywhere, anywhere, pl.BlockSpec(memory_space=pltpu.SMEM), anywhere],
+        in_specs=[anywhere] * 4,
         out_specs=vmem,
         scratch_shapes=[
+            pltpu.SMEM(cheb_coefs.shape, cheb_coefs.dtype),
             pltpu.VMEM(features.shape, features.dtype),
             pltpu.VMEM(merging_weight.shape, merging_weight.dtype),
             pltpu.VMEM(dense.shape, dense.dtype),
@@ -240,6 +266,7 @@
             pltpu.VMEM((rels, rel_count, part, width), half),
             pltpu.VMEM((rel_count, rels, part, width), half),
             dma((rels,)),
+            dma,
             dma,
             dma,
             dma((ORDERS, rels, row_count)),

time: 79.7 us -> 79.1 us (level)
  no operation moved by 1% of the time
where the time goes in v3:
time: 79.1 us; the launch traced here: 79 us
  Pallas kernels  71.4 us (90%)
  local copies, waits for them, and re-layouts  7.6 us (10%)
    pallas_call x1, Pallas kernels, local(): pl.pallas_call(functools.partial(propagate_kernel, row_count, col_count,...  67.2 us
    unnamed x11, local copies, waits for them, and re-layouts  7.6 us
    pallas_call x1, Pallas kernels, assemble(): pl.pallas_call(assemble_kernel, grid=(rels, col_count), out_shape=jax.Sha...  4.14 us

profile of v3, /device:TPU:0, one launch (start us, length us, event | category | flops | bytes accessed | tf_op | source)
XLA Modules:
  0.0 79.0 jit_solution(3282468593535216762)
XLA Ops:
  0.0 0.0 copy-start.1
  0.0 2.2 %copy-done.1 = bf16[2,1,1,16,256,256]{5,4,3,2,1,0:T(8,128)(2,1)S(1)} copy-done((bf16[2,1,1,16,256,256]{5,4,3,2,1,0:T(8,128)(2,1)S(1)}, bf16[2,1,1,16,256,256]{5,4,3,2,1,0:T(8,128)(2,1)}, u32[]{:S(2)}) %copy-start.1) | copy-done | bytes 4194328
  2.2 0.0 copy-start.2
  2.2 0.7 copy-done.2
  2.9 0.0 copy-start.3
  2.9 0.7 copy-done.3
  3.5 0.0 copy-start.4
  3.5 0.7 copy-done.4
  4.2 4.1 %shard_map.73.dense_ref = bf16[2,4,256,1024]{3,2,1,0:T(8,128)(2,1)S(1)} custom-call(s32[2,16]{1,0:T(2,128)S(1)} %bitcast.5, s32[2,16]{1,0:T(2,128)S(1)} %bitcast.6, s32[2]{0:T(128)S(1)} %bitcast.7, bf16[2,16,256,256]{3,2,1,0:T(8,128)(2,1)S(1)} %bitcast.4), custom_call_target="tpu_custom_call" | custom-call | tf_op jit(solution)/shard_map/pallas_call | solution.py:51
  8.3 0.0 copy-start
  8.4 1.9 %copy-done = bf16[2,4,256,1024]{3,2,1,0:T(8,128)(2,1)} copy-done((bf16[2,4,256,1024]{3,2,1,0:T(8,128)(2,1)}, bf16[2,4,256,1024]{3,2,1,0:T(8,128)(2,1)S(1)}, u32[]{:S(2)}) %copy-start) | copy-done | bytes 4194328
  10.3 67.2 %shard_map.74 = f32[1,128,128]{2,1,0:T(8,128)} custom-call(f32[2,1,256,128]{3,2,1,0:T(8,128)} %features_hbm.1, bf16[2,4,256,1024]{3,2,1,0:T(8,128)(2,1)} %copy-done, f32[2,5]{1,0:T(2,128)} %coefs_hbm.1, bf16[512,128]{1,0:T(8,128)(2,1)} %weight_hbm.1), custom_call_target="tpu_custom_call" | custom-call | tf_op jit(solution)/shard_map/pallas_call | solution.py:249
  77.5 1.5 %copy.9 = f32[1,128,128]{2,1,0:T(8,128)} copy(f32[1,128,128]{2,1,0:T(8,128)} %shard_map.74) | data formatting | bytes 131072
Async XLA Ops:
  0.0 2.2 %copy-start.1 = (bf16[2,1,1,16,256,256]{5,4,3,2,1,0:T(8,128)(2,1)S(1)}, bf16[2,1,1,16,256,256]{5,4,3,2,1,0:T(8,128)(2,1)}, u32[]{:S(2)}) copy-start(bf16[2,1,1,16,256,256]{5,4,3,2,1,0:T(8,128)(2,1)} %param.8) | copy-start | bytes 12582916
  2.2 0.7 copy-start.2
  2.9 0.7 copy-start.3
  3.5 0.7 copy-start.4
  8.3 1.9 %copy-start = (bf16[2,4,256,1024]{3,2,1,0:T(8,128)(2,1)}, bf16[2,4,256,1024]{3,2,1,0:T(8,128)(2,1)S(1)}, u32[]{:S(2)}) copy-start(bf16[2,4,256,1024]{3,2,1,0:T(8,128)(2,1)S(1)} %shard_map.73.dense_ref) | copy-start | bytes 12582916
